TPU v7x, 128 devices: a whole 4x4x4 slice. The times are simulated.
128 devices in a mesh: wide: 8 (over y_lo, z), narrow: 16 (over y_hi, x, core).
Axes of the slice: x: 4, y: 4 (y_hi: 2, y_lo: 2; y = y_hi * 2 + y_lo), z: 4, core: 2. Of those that a mesh axis runs over, the one named last changes fastest.
Arguments:
- saved_inputs: bfloat16 [2048, 5120], P('wide', 'narrow'), may hold values from -6 to 6
- out_grads: bfloat16 [2048, 5120], P('wide', 'narrow'), may hold values from -48 to 48
- seq_ids: int32 [2048], P('wide'), may hold values from 0 to 15, as said below
- seq_counts: int32 [16], P('wide'), may hold values from 64 to 192, as said below
- basis_in: bfloat16 [5120, 5120], P('narrow'), may hold values from -0.078125 to 0.078125
- basis_out: bfloat16 [5120, 5120], P('narrow'), may hold values from -0.078125 to 0.078125
- query_rotated: bfloat16 [5120, 5120], P('narrow', 'wide'), may hold values from -6 to 6
- damping: float32 [], replicated, may hold values from 0.05 to 0.5
Outputs:
- eigenvalues: float32 [5120, 5120], P('narrow', 'wide')
- preconditioned: float32 [5120, 5120], P('narrow', 'wide')
Inputs may be any that keep to these rules, and one draw needn't show every extreme that they name: seq_ids names for each token its sequence; the 256 tokens of block w of the token axis belong to the sequences 2 * w to 2 * w + 1, each having at least one token. seq_counts[s] is the number of tokens whose seq_ids equal s.
All inputs are finite; a program needn't handle non-finite values.
Results may differ from a plain program's by a relative error of at most 0.01.
Values may be sent and summed in bfloat16 or wider, within the bound.
A program may use at most 128 MiB of HBM per device.

v0:
```python
import jax
import jax.numpy as jnp
from jax import lax
from jax.sharding import PartitionSpec as P


def in_order(pieces, dim):
    pieces = jnp.moveaxis(pieces, 0, dim)
    shape = pieces.shape
    return pieces.reshape(*shape[:dim], shape[dim] * shape[dim + 1], *shape[dim + 2 :])


def copy_for_each(value, axis):
    copies = jnp.broadcast_to(value, (lax.axis_size(axis), *value.shape))
    return lax.all_to_all(copies, axis, split_axis=0, concat_axis=0, tiled=True)


def collect(value, axis, dim):
    return in_order(copy_for_each(value, axis), dim)


def in_one_piece(arrays, axis, dim, along):
    widths = [a.shape[along] for a in arrays]
    both = jnp.concatenate(arrays, axis=along)
    whole = lax.all_gather(both, axis, axis=dim, tiled=True)
    return tuple(jnp.split(whole, [sum(widths[:k]) for k in range(1, len(widths))], axis=along))


def shards(
    saved_inputs, out_grads, seq_ids, seq_counts, basis_in, basis_out, query_rotated, damping
):
    part_in = jnp.dot(saved_inputs, basis_in, preferred_element_type=jnp.float32)
    part_grad = jnp.dot(out_grads, basis_out, preferred_element_type=jnp.float32)
    rot_in = lax.psum(part_in, "narrow").astype(jnp.bfloat16)
    rot_grad = lax.psum_scatter(part_grad, "narrow", scatter_dimension=1, tiled=True).astype(
        jnp.bfloat16
    )
    seq_local = seq_counts.shape[0]
    tok_local = seq_ids.shape[0]
    offset = lax.axis_index("wide") * seq_local
    member = seq_ids[None, :] - offset == jnp.arange(seq_local, dtype=jnp.int32)[:, None]
    weight = (
        jnp.where(member, 1.0, 0.0).astype(jnp.float32) / seq_counts.astype(jnp.float32)[:, None]
    )
    weighted = (rot_grad.astype(jnp.float32)[None, :, :] * weight[:, :, None]).astype(jnp.bfloat16)
    total_seqs = seq_local * lax.axis_size("wide")
    groups = lax.axis_size("wide")
    all_weighted = collect(weighted, "wide", 0)
    all_weighted = all_weighted.reshape(groups, seq_local, tok_local, all_weighted.shape[2])
    column_rows = lax.all_to_all(rot_in, "wide", split_axis=1, concat_axis=0, tiled=True)
    column_rows = column_rows.reshape(groups, tok_local, column_rows.shape[1])
    per_seq = jnp.einsum(
        "gsti,gtj->gsij", all_weighted, column_rows, preferred_element_type=jnp.float32
    )
    eigenvalues = jnp.sum(per_seq * per_seq, axis=(0, 1)) / total_seqs
    scaled = (query_rotated.astype(jnp.float32) / (eigenvalues + damping)).astype(jnp.bfloat16)
    width = query_rotated.shape[1]
    in_columns = lax.dynamic_slice_in_dim(basis_in, lax.axis_index("wide") * width, width, 1)
    all_scaled, all_columns = in_one_piece((scaled, in_columns), "narrow", 0, 1)
    middle = jnp.dot(basis_out, all_scaled, preferred_element_type=jnp.float32).astype(jnp.bfloat16)
    partial_back = lax.dot_general(
        middle, all_columns, (((1,), (1,)), ((), ())), preferred_element_type=jnp.float32
    )
    preconditioned = lax.psum_scatter(partial_back, "wide", scatter_dimension=1, tiled=True)
    return (eigenvalues, preconditioned)


def solution(mesh):
    return jax.shard_map(
        shards,
        mesh=mesh,
        in_specs=(
            P("wide", "narrow"),
            P("wide", "narrow"),
            P("wide"),
            P("wide"),
            P("narrow", None),
            P("narrow", None),
            P("narrow", "wide"),
            P(),
        ),
        out_specs=(P("narrow", "wide"), P("narrow", "wide")),
        check_vma=False,
    )
```

profile of v0, /device:TPU:1, one launch (start us, length us, event | category | flops | bytes accessed | tf_op | source)
XLA Modules:
  0.0 396.9 jit_solution(1464753406761184582)
XLA Ops:
  7.2 0.0 copy-start
  7.2 0.0 reduce-scatter.3.cloned.1.call-start
  7.2 1.9 copy-done
  9.1 5.0 %fusion.11 = f32[256,5120]{0,1:T(8,128)} fusion(bf16[256,320]{0,1:T(8,128)(2,1)} %param.9, bf16[320,5120]{1,0:T(8,128)(2,1)S(1)} %copy-done), kind=kOutput, calls=%fused_computation.17 | convolution fusion | flops 838860800 | bytes 8683520 | tf_op jit(solution)/shard_map/dot_general | solution.py:33
  14.1 0.0 copy-start.3
  14.1 0.0 reduce-scatter.3.cloned.1.call-update
  14.2 0.9 copy-done.3
  15.0 5.8 %fusion.12 = f32[256,5120]{1,0:T(8,128)} fusion(bf16[256,320]{0,1:T(8,128)(2,1)S(1)} %copy-done.3, bf16[320,5120]{1,0:T(8,128)(2,1)} %param.12), kind=kOutput, calls=%fused_computation.18 | convolution fusion | flops 838860800 | bytes 8683520 | tf_op jit(solution)/shard_map/dot_general | solution.py:32
  20.9 100.9 %all-reduce.1 = bf16[256,5120]{1,0:T(8,128)(2,1)} all-reduce(f32[256,5120]{1,0:T(8,128)} %fusion.12), channel_id=1, replica_groups=mesh['wide'=8,'narrow'=16] {'narrow'}, use_global_device_ids=true, to_apply=%region_1.0 | all-reduce | flops 1310720 | bytes 7864320 | tf_op jit(solution)/shard_map/psum | solution.py:34
  121.8 3.5 copy.14
  125.3 0.0 copy-start.5
  125.3 0.0 copy-start.4
  125.3 9.7 %all-to-all-start.1 = ((bf16[256,8,640]{2,0,1:T(8,128)(2,1)}), bf16[256,8,640]{2,0,1:T(8,128)(2,1)}, u32[]{:S(2)}, u32[]{:S(2)}) async-start(bf16[256,8,640]{2,0,1:T(8,128)(2,1)} %bitcast.17), calls=%async_computation.2 | async-start | bytes 5242880 | tf_op jit(solution)/shard_map/all_to_all | solution.py:50
  135.0 0.0 copy-done.5
  135.0 0.0 copy-done.4
  135.1 0.1 fusion.10
  135.1 0.0 reduce-scatter.3.cloned.1.call-done
  135.1 1.0 convert_convert_fusion
  136.1 0.8 multiply_convert_fusion
  136.9 30.0 %all-to-all-done.1 = bf16[256,8,640]{2,0,1:T(8,128)(2,1)} async-done(((bf16[256,8,640]{2,0,1:T(8,128)(2,1)}), bf16[256,8,640]{2,0,1:T(8,128)(2,1)}, u32[]{:S(2)}, u32[]{:S(2)}) %all-to-all-start.1) | async-done | bytes 2621472 | tf_op jit(solution)/shard_map/all_to_all | solution.py:50
  167.0 2.7 broadcast_in_dim.18
  169.7 4.4 %all-to-all-start = ((bf16[8,2,256,320]{2,3,1,0:T(8,128)(2,1)}), bf16[8,2,256,320]{2,3,1,0:T(8,128)(2,1)}, u32[]{:S(2)}, u32[]{:S(2)}) async-start(bf16[8,2,256,320]{2,3,1,0:T(8,128)(2,1)} %broadcast_in_dim.18), calls=%async_computation.1 | async-start | bytes 5242880 | tf_op jit(solution)/shard_map/all_to_all | solution.py:15
  174.1 0.0 all-gather.2.cloned.1.call-start
  174.8 1.8 constant_dynamic-slice_fusion
  176.6 29.3 %all-to-all-done = bf16[8,2,256,320]{2,3,1,0:T(8,128)(2,1)} async-done(((bf16[8,2,256,320]{2,3,1,0:T(8,128)(2,1)}), bf16[8,2,256,320]{2,3,1,0:T(8,128)(2,1)}, u32[]{:S(2)}, u32[]{:S(2)}) %all-to-all-start) | async-done | bytes 2621472 | tf_op jit(solution)/shard_map/all_to_all | solution.py:15
  205.9 0.0 copy-start.2
  205.9 0.0 copy-start.1
  205.9 4.9 %multiply_reduce_fusion = f32[320,640]{1,0:T(8,128)S(1)} fusion(bf16[8,2,256,320]{2,3,1,0:T(8,128)(2,1)} %all-to-all-done, bf16[256,8,640]{2,0,1:T(8,128)(2,1)} %all-to-all-done.1), kind=kOutput, calls=%fused_computation | convolution fusion | flops 1684070400 | bytes 6062080 | tf_op jit(solution)/shard_map/gsti,gtj->gsij/dot_general | solution.py:52
  210.8 0.0 copy-done.2
  210.8 1.0 divide_convert_fusion
  211.8 0.0 copy-done.1
  211.8 1.0 pad_maximum_fusion
  212.8 0.0 all-gather.2.cloned.1.call-update
  212.8 0.2 reduce-scatter.5.cloned.1.call-start
  213.0 90.6 %all-gather.2.cloned.1.call-done = bf16[5120,1280]{1,0:T(8,128)(2,1)} async-done(((bf16[320,1280]{1,0:T(8,128)(2,1)}), bf16[5120,1280]{1,0:T(8,128)(2,1)}) %all-gather.2.cloned.1.call-update) | async-done | bytes 13107216 | tf_op jit(solution)/shard_map/all_gather | solution.py:25
  303.6 13.7 %fusion = f32[320,5120]{1,0:T(8,128)} fusion(bf16[5120,1280]{1,0:T(8,128)(2,1)} %all-gather.2.cloned.1.call-done, bf16[320,5120]{1,0:T(8,128)(2,1)S(1)} %copy-done), kind=kOutput, calls=%fused_computation.1 | convolution fusion | flops 4194508800 | bytes 22937600 | tf_op jit(solution)/shard_map/dot_general | solution.py:61
  317.3 0.0 reduce-scatter.5.cloned.1.call-update
  317.3 73.1 %reduce-scatter.5.cloned.1.call-done = f32[320,640]{1,0:T(8,128)} async-done(((f32[320,5120]{1,0:T(8,128)}), f32[320,640]{1,0:T(8,128)}) %reduce-scatter.5.cloned.1.call-update) | async-done | bytes 819216 | tf_op jit(solution)/shard_map/reduce_scatter | solution.py:64
  (2 shorter events, 0.0 us)
Async XLA Ops:
  7.2 1.9 copy-start
  7.2 128.0 %reduce-scatter.3.cloned.1.call-start = ((), (), s32[]{:S(2)}) async-start(), calls=%async_computation.4 | async-start | bytes 5570560 | tf_op jit(solution)/shard_map/reduce_scatter | solution.py:35
  14.1 0.9 copy-start.3
  125.3 9.7 %copy-start.5 = (s32[2]{0:T(128)S(1)}, s32[2]{0:T(128)}, u32[]{:S(2)}) copy-start(s32[2]{0:T(128)} %param.11) | copy-start | bytes 28
  125.3 9.7 %copy-start.4 = (s32[256]{0:T(256)S(1)}, s32[256]{0:T(256)}, u32[]{:S(2)}) copy-start(s32[256]{0:T(256)} %param.10) | copy-start | bytes 3076
  125.3 41.6 %all-to-all-start.1 = ((bf16[256,8,640]{2,0,1:T(8,128)(2,1)}), bf16[256,8,640]{2,0,1:T(8,128)(2,1)}, u32[]{:S(2)}, u32[]{:S(2)}) async-start(bf16[256,8,640]{2,0,1:T(8,128)(2,1)} %bitcast.17), calls=%async_computation.2 | async-start | bytes 5242880 | tf_op jit(solution)/shard_map/all_to_all | solution.py:50
  169.7 36.2 %all-to-all-start = ((bf16[8,2,256,320]{2,3,1,0:T(8,128)(2,1)}), bf16[8,2,256,320]{2,3,1,0:T(8,128)(2,1)}, u32[]{:S(2)}, u32[]{:S(2)}) async-start(bf16[8,2,256,320]{2,3,1,0:T(8,128)(2,1)} %broadcast_in_dim.18), calls=%async_computation.1 | async-start | bytes 5242880 | tf_op jit(solution)/shard_map/all_to_all | solution.py:15
  174.1 129.5 %all-gather.2.cloned.1.call-start = ((), (), s32[]{:S(2)}) async-start(), calls=%async_computation.5 | async-start | bytes 13926400 | tf_op jit(solution)/shard_map/all_gather | solution.py:25
  205.9 4.9 %copy-start.2 = (bf16[320,640]{1,0:T(8,128)(2,1)S(1)}, bf16[320,640]{1,0:T(8,128)(2,1)}, u32[]{:S(2)}) copy-start(bf16[320,640]{1,0:T(8,128)(2,1)} %param.14) | copy-start | bytes 1228804
  205.9 5.9 %copy-start.1 = (bf16[320,640]{1,0:T(8,128)(2,1)S(1)}, bf16[320,640]{1,0:T(8,128)(2,1)}, u32[]{:S(2)}) copy-start(bf16[320,640]{1,0:T(8,128)(2,1)} %constant_dynamic-slice_fusion) | copy-start | bytes 1228804
  212.8 177.5 %reduce-scatter.5.cloned.1.call-start = ((), (), s32[]{:S(2)}) async-start(), calls=%async_computation.6 | async-start | bytes 7372800 | tf_op jit(solution)/shard_map/reduce_scatter | solution.py:64
Sparse Core Ops, SparseCore 0:
  14.3 107.6 reduce-scatter.2
  212.9 90.6 all-gather.1
  317.4 72.8 reduce-scatter.4
where the time goes:
time: 397 us
  waiting for transfers between devices  223 us (56%)
  blocking collectives  101 us (25%)
  matrix products  29.4 us (7%)
  between operations  14.5 us (4%)
  starting transfers between devices  14.4 us (4%)
  local copies, waits for them, and re-layouts  10.9 us (3%)
    psum x1, blocking collectives, shards(): rot_in = lax.psum(part_in, 'narrow').astype(jnp.bfloat16)  101 us
    all_gather x1, waiting for transfers between devices, in_one_piece(): whole = lax.all_gather(both, axis, axis=dim, tiled=True)  90.6 us
    reduce_scatter x1, waiting for transfers between devices, shards(): lax.psum_scatter(partial_back, 'wide', scatter_dimension=1, tiled=True)  73.1 us
    all_to_all x1, waiting for transfers between devices, shards(): lax.all_to_all(rot_in, 'wide', split_axis=1, concat_axis=0, tiled=True)  30 us
    all_to_all x1, waiting for transfers between devices, copy_for_each(): return lax.all_to_all(copies, axis, split_axis=0, concat_axis=0, tiled=True)  29.3 us
    dot_general x1, matrix products, shards(): lax.dot_general(middle, all_columns, (((1,), (1,)), ((), ())), preferred_...  13.7 us
    all_to_all x1, starting transfers between devices, shards(): lax.all_to_all(rot_in, 'wide', split_axis=1, concat_axis=0, tiled=True)  9.72 us
  transfers between devices with their start and end apart: 5, of which 4 were waited for; matrix products, arithmetic and copies ran while one was open for 3% of the time, Pallas kernels for 0%

commit v1 on v0

v1 whole, which is shorter than its diff:
```python
import jax
import jax.numpy as jnp
from jax import lax
from jax.experimental import pallas as pl
from jax.experimental.pallas import tpu as pltpu
from jax.sharding import PartitionSpec as P

MESH = pl.DeviceIdType.MESH
BF = jnp.bfloat16
F32 = jnp.float32

D = 5120
TOK = 256
NB = 320
WB = 640
SUB = 16
GROWS = NB + 16
NSEM = 192


def kernel(
    x_ref, g_ref, ids_ref, cnt_ref, damp_ref, q_ref, bin_hbm, bout_hbm,
    eig_ref, out_ref,
    bout, incols, xw, pt, ps, rh, rf, ry, ryb, gt, rot, rotacc, sall, acc, mid, pb, eh, ef, ey, eyb,
    ssem, rsem, lsem,
):
    w = lax.axis_index("wide")
    n = lax.axis_index("narrow")
    yl, z = w // 4, w % 4
    yh, x, k = n // 8, (n // 2) % 4, n % 2

    def nslot(dx, dy):
        return (yh + dy) % 2 * 8 + (x + dx) % 4 * 2 + k

    def wslot(dz, dy):
        return (yl + dy) % 2 * 4 + (z + dz) % 4

    def cslot(dx, dy):
        return (yh + dy) % 2 * 4 + (x + dx) % 4

    sib = (w, n + 1 - 2 * k)
    xr, xl, yp = (w, nslot(1, 0)), (w, nslot(3, 0)), (w, nslot(0, 1))
    zr, zl, yq = (wslot(1, 0), n), (wslot(3, 0), n), (wslot(0, 1), n)
    ynb = (wslot(0, 1), nslot(0, 1))

    count = [0]
    sent = []

    def send(src, dst, to):
        c = count[0]
        count[0] += 1
        copy = pltpu.make_async_remote_copy(
            src_ref=src, dst_ref=dst, send_sem=ssem.at[c], recv_sem=rsem.at[c],
            device_id=to, device_id_type=MESH,
        )
        copy.start()
        sent.append(copy)
        return copy

    load_bout = pltpu.make_async_copy(bout_hbm, bout, lsem.at[0])
    load_bout.start()
    mine = pl.ds(pl.multiple_of(w * WB, 128), WB)
    load_cols = pltpu.make_async_copy(bin_hbm.at[:, mine], incols.at[n], lsem.at[1])
    load_cols.start()

    barrier = pltpu.get_barrier_semaphore()
    others = [(w, (n + d) % 16) for d in range(1, 16)]
    for to in others + [zr, zl, yq, ynb]:
        pl.semaphore_signal(barrier, inc=1, device_id=to, device_id_type=MESH)
    pl.semaphore_wait(barrier, len(others) + 4)

    class Gather:
        def __init__(self, view, half, slot, right, left, part, to_sib):
            self.view, self.half, self.slot = view, half, slot
            self.right, self.left, self.part, self.to_sib = right, left, part, to_sib
            self.sibs = []

        def fwd(self, dx, dy):
            if self.to_sib:
                v = self.view(self.slot(dx, dy))
                self.sibs.append(send(v, v, sib))

        def hop(self, v, to):
            return send(v, v, to)

        def start(self, src=None, part_src=None):
            v = self.view(self.slot(0, 0))
            src = v if src is None else src
            self.r = send(src, v, self.right)
            self.l = send(src, v, self.left)
            self.p = send(src if part_src is None else part_src, v, self.part)
            if self.to_sib:
                self.sibs.append(send(src, v, sib))

        def near(self):
            self.r.wait_recv()
            self.fr = self.hop(self.half(self.slot(3, 0), 0), self.right)
            self.fwd(3, 0)
            self.l.wait_recv()
            self.fl = self.hop(self.half(self.slot(1, 0), 1), self.left)
            self.fwd(1, 0)

        def across(self):
            self.p.wait_recv()
            v = self.view(self.slot(0, 1))
            self.pr = self.hop(v, self.right)
            self.pl = self.hop(v, self.left)
            self.fwd(0, 1)

        def far(self):
            self.fr.wait_recv()
            self.fl.wait_recv()
            self.fwd(2, 0)

        def across_near(self):
            self.pr.wait_recv()
            self.pfr = self.hop(self.half(self.slot(3, 1), 0), self.right)
            self.fwd(3, 1)
            self.pl.wait_recv()
            self.pfl = self.hop(self.half(self.slot(1, 1), 1), self.left)
            self.fwd(1, 1)

        def across_far(self):
            self.pfr.wait_recv()
            self.pfl.wait_recv()
            self.fwd(2, 1)

        def got_sib(self, i):
            self.sibs[i].wait_recv()

    class Scatter:
        def __init__(self, view, half, slot, right, left, part, h, f, fy, fyb):
            self.view, self.half, self.slot = view, half, slot
            self.right, self.left, self.part = right, left, part
            self.h, self.f, self.fy, self.fyb = h, f, fy, fyb
            self.one, self.two = {}, {}

        def first(self, y):
            c = self.slot(2, y)
            self.one[y] = (
                send(self.half(c, 1), self.h.at[y, 0], self.right),
                send(self.half(c, 0), self.h.at[y, 1], self.left),
            )

        def second(self, y):
            for d, (dx, part, to) in enumerate(((1, 1, self.right), (3, 0, self.left))):
                self.one[y][d].wait_recv()
                v = self.half(self.slot(dx, y), part)
                v[...] = (v[...].astype(F32) + self.h[y, d].astype(F32)).astype(BF)
                copy = send(self.view(self.slot(dx, y)), self.f.at[y, d], to)
                self.two[y] = self.two.get(y, ()) + (copy,)

        def total(self, y):
            for copy in self.two[y]:
                copy.wait_recv()
            own = self.view(self.slot(0, y))
            return own[...].astype(F32) + self.f[y, 0].astype(F32) + self.f[y, 1].astype(F32)

        def third(self):
            self.fyb[...] = self.total(1).astype(BF)
            self.last = send(self.fyb, self.fy, self.part)

        def fourth(self):
            t = self.total(0)
            self.last.wait_recv()
            return t + self.fy[...].astype(F32)

    theirs = pl.ds(pl.multiple_of(wslot(0, 1) * WB, 128), WB)
    cols = Gather(
        lambda s: incols.at[s], lambda s, h: incols.at[s, pl.ds(160 * h, 160)],
        nslot, xr, xl, ynb, True,
    )
    cols.start(bin_hbm.at[:, mine], bin_hbm.at[:, theirs])

    put_x = []
    for to in others:
        rows = pl.ds(pl.multiple_of(to[1] * SUB, SUB), SUB)
        put_x.append(send(x_ref.at[rows], xw.at[w, n], to))
    xw[w, n] = x_ref[pl.ds(pl.multiple_of(n * SUB, SUB), SUB), :]

    load_bout.wait()

    def rotate_grad(c, _):
        at = pl.ds(pl.multiple_of(c * WB, 128), WB)
        part = jnp.dot(g_ref[...], bout[:, at], preferred_element_type=F32).T
        pt[0, c] = part[:NB].astype(BF)
        pt[1, c] = part[NB:].astype(BF)
        return _

    lax.fori_loop(0, 8, rotate_grad, 0)
    swap = send(pt.at[1 - k], ps, sib)

    for copy in put_x:
        copy.wait_recv()
    xg = Gather(
        lambda s: xw.at[s], lambda s, h: xw.at[s, pl.ds(8 * h, 8)], wslot, zr, zl, yq, False
    )
    xg.start()

    swap.wait_recv()
    grads = Scatter(
        lambda c: ps.at[c], lambda c, h: ps.at[c, pl.ds(160 * h, 160)],
        cslot, xr, xl, yp, rh, rf, ry, ryb,
    )

    def both(dx, dy):
        c = cslot(dx, dy)
        ps[c] = (ps[c].astype(F32) + pt[k, c].astype(F32)).astype(BF)

    both(2, 1)
    grads.first(1)
    both(2, 0)
    grads.first(0)
    for dy in (1, 0):
        for dx in (1, 3, 0):
            both(dx, dy)

    cols.near()
    xg.near()
    xg.across()
    grads.second(1)
    grads.second(0)
    cols.across()
    xg.far()
    xg.across_near()
    grads.third()
    xg.across_far()
    load_cols.wait()

    def rotate_in(dx, dy, first=False):
        total = None
        for core in range(2):
            s = cslot(dx, dy) * 2 + core
            part = jnp.dot(
                xw[:, s].reshape(8 * SUB, NB), incols[s], preferred_element_type=F32
            )
            total = part if total is None else total + part
        rotacc[...] = total if first else rotacc[...] + total

    cols.got_sib(0)
    rotate_in(0, 0, True)
    cols.far()
    rotg = grads.fourth()

    is_first = ids_ref[...] == 2 * w
    count_of = jnp.where(
        is_first, jnp.broadcast_to(cnt_ref[:, 0:1], (1, TOK)), jnp.broadcast_to(cnt_ref[:, 1:2], (1, TOK))
    )
    weight = 1.0 / count_of.astype(F32)
    gt[w, :NB] = (rotg.astype(BF).astype(F32) * weight).astype(BF)
    gt[w, NB:] = jnp.broadcast_to(jnp.where(is_first, 1.0, 0.0).astype(BF), (16, TOK))
    gg = Gather(
        lambda s: gt.at[s],
        lambda s, h: gt.at[s, pl.ds(176 * h, 176 - 16 * h)],
        wslot, zr, zl, yq, False,
    )
    gg.start()

    cols.got_sib(1)
    rotate_in(3, 0)
    cols.got_sib(2)
    rotate_in(1, 0)
    cols.across_near()
    cols.got_sib(3)
    rotate_in(0, 1)
    cols.got_sib(4)
    rotate_in(2, 0)
    gg.near()
    cols.got_sib(5)
    rotate_in(3, 1)
    cols.got_sib(6)
    rotate_in(1, 1)
    cols.across_far()
    cols.got_sib(7)
    rotate_in(2, 1)

    rot[:, pl.ds(pl.multiple_of(n * SUB, SUB), SUB), :] = (
        rotacc[...].astype(BF).reshape(8, SUB, WB)
    )

    def rows_of(s):
        return pl.ds(pl.multiple_of(s * SUB, SUB), SUB)

    rg = Gather(
        lambda s: rot.at[:, rows_of(s)],
        lambda s, h: rot.at[pl.ds(4 * h, 4), rows_of(s)],
        nslot, xr, xl, yp, True,
    )
    rg.start()
    gg.across()
    rg.near()
    rg.across()
    gg.far()
    gg.across_near()
    rg.far()
    rg.across_near()
    gg.across_far()
    rg.across_far()
    for i in range(8):
        rg.got_sib(i)

    acc[...] = jnp.zeros_like(acc)

    def fit(b, _):
        grad = gt[b, :NB]
        mask = gt[b, NB:NB + 1]
        one = grad * mask
        rows = rot[b]
        p = jnp.dot(one, rows, preferred_element_type=F32)
        r = jnp.dot(grad - one, rows, preferred_element_type=F32)
        acc[...] += p * p + r * r
        return _

    lax.fori_loop(0, 8, fit, 0)
    eig = acc[...] * (1.0 / 16)
    eig_ref[...] = eig
    sall[n] = (q_ref[...].astype(F32) / (eig + damp_ref[...])).astype(BF)

    sg = Gather(
        lambda s: sall.at[s], lambda s, h: sall.at[s, pl.ds(160 * h, 160)],
        nslot, xr, xl, yp, True,
    )
    sg.start()

    def rotate_out(dx, dy, first=False):
        c = cslot(dx, dy)
        at = pl.ds(pl.multiple_of(c * WB, 128), WB)
        part = jnp.dot(
            bout[:, at], sall[pl.ds(2 * c, 2)].reshape(WB, WB), preferred_element_type=F32
        )
        acc[...] = part if first else acc[...] + part

    sg.got_sib(0)
    rotate_out(0, 0, True)
    sg.near()
    sg.got_sib(1)
    rotate_out(3, 0)
    sg.got_sib(2)
    rotate_out(1, 0)
    sg.across()
    sg.far()
    sg.got_sib(3)
    rotate_out(0, 1)
    sg.got_sib(4)
    rotate_out(2, 0)
    sg.across_near()
    sg.got_sib(5)
    rotate_out(3, 1)
    sg.got_sib(6)
    rotate_out(1, 1)
    sg.across_far()
    sg.got_sib(7)
    rotate_out(2, 1)
    mid[...] = acc[...].astype(BF)

    def back(dz, dy):
        s = wslot(dz, dy)
        pb[s] = lax.dot_general(
            mid[...], incols[pl.ds(2 * s, 2)].reshape(WB, WB), (((1,), (1,)), ((), ())),
            preferred_element_type=F32,
        ).astype(BF)

    es = Scatter(
        lambda s: pb.at[s], lambda s, h: pb.at[s, pl.ds(160 * h, 160)],
        wslot, zr, zl, yq, eh, ef, ey, eyb,
    )
    back(2, 1)
    es.first(1)
    back(2, 0)
    es.first(0)
    for dy in (1, 0):
        for dz in (1, 3, 0):
            back(dz, dy)
    es.second(1)
    es.second(0)
    es.third()
    out_ref[...] = es.fourth()

    for copy in sent:
        copy.wait_send()


def shards(
    saved_inputs, out_grads, seq_ids, seq_counts, basis_in, basis_out, query_rotated, damping
):
    vm = pl.BlockSpec(memory_space=pltpu.VMEM)
    hbm = pl.BlockSpec(memory_space=pl.ANY)
    tile = jax.ShapeDtypeStruct((NB, WB), F32)
    return pl.pallas_call(
        kernel,
        out_shape=(tile, tile),
        in_specs=[vm] * 6 + [hbm] * 2,
        out_specs=(vm, vm),
        scratch_shapes=[
            pltpu.VMEM((NB, D), BF),
            pltpu.VMEM((16, NB, WB), BF),
            pltpu.VMEM((8, 16, SUB, NB), BF),
            pltpu.VMEM((2, 8, NB, TOK), BF),
            pltpu.VMEM((8, NB, TOK), BF),
            pltpu.VMEM((2, 2, NB // 2, TOK), BF),
            pltpu.VMEM((2, 2, NB, TOK), BF),
            pltpu.VMEM((NB, TOK), BF),
            pltpu.VMEM((NB, TOK), BF),
            pltpu.VMEM((8, GROWS, TOK), BF),
            pltpu.VMEM((8, TOK, WB), BF),
            pltpu.VMEM((8 * SUB, WB), F32),
            pltpu.VMEM((16, NB, WB), BF),
            pltpu.VMEM((NB, WB), F32),
            pltpu.VMEM((NB, WB), BF),
            pltpu.VMEM((8, NB, WB), BF),
            pltpu.VMEM((2, 2, NB // 2, WB), BF),
            pltpu.VMEM((2, 2, NB, WB), BF),
            pltpu.VMEM((NB, WB), BF),
            pltpu.VMEM((NB, WB), BF),
            pltpu.SemaphoreType.DMA((NSEM,)),
            pltpu.SemaphoreType.DMA((NSEM,)),
            pltpu.SemaphoreType.DMA((2,)),
        ],
        compiler_params=pltpu.CompilerParams(
            collective_id=0, has_side_effects=True, vmem_limit_bytes=60 * 1024 * 1024
        ),
    )(
        saved_inputs, out_grads, seq_ids.reshape(1, -1), seq_counts.reshape(1, -1),
        damping.reshape(1, 1), query_rotated, basis_in, basis_out,
    )


def solution(mesh):
    return jax.shard_map(
        shards,
        mesh=mesh,
        in_specs=(
            P("wide", "narrow"),
            P("wide", "narrow"),
            P("wide"),
            P("wide"),
            P("narrow", None),
            P("narrow", None),
            P("narrow", "wide"),
            P(),
        ),
        out_specs=(P("narrow", "wide"), P("narrow", "wide")),
        check_vma=False,
    )
```

time: 397 us -> 159 us (0.40)
  waiting for transfers between devices: 223 us -> 0 us
  Pallas kernels: 0 us -> 149 us
  blocking collectives: 101 us -> 0 us
  matrix products: 29.4 us -> 0 us
  starting transfers between devices: 14.4 us -> 0 us
  between operations: 14.5 us -> 1.29 us
    pallas_call x0 -> x1, Pallas kernels: none -> 149 us  [shards(): pl.pallas_call(kernel, out_shape=(tile, tile), in_specs=[vm] * 6 + [hbm]...]
    psum x1 -> x0, blocking collectives: 101 us -> none  [shards(): rot_in = lax.psum(part_in, 'narrow').astype(jnp.bfloat16)]
    all_gather x1 -> x0, waiting for transfers between devices: 90.6 us -> none  [in_one_piece(): whole = lax.all_gather(both, axis, axis=dim, tiled=True)]
    reduce_scatter x2 -> x0, waiting for transfers between devices: 73.1 us -> none  [the longest x1 73.1 us: shards(): lax.psum_scatter(partial_back, 'wide', scatter_dimension=1, tiled=True)]
    all_to_all x2 -> x0, waiting for transfers between devices: 59.3 us -> none  [the longest x1 30 us: shards(): lax.all_to_all(rot_in, 'wide', split_axis=1, concat_axis=0, tiled=True)]
    dot_general x4 -> x0, matrix products: 29.4 us -> none  [the longest x1 13.7 us: shards(): lax.dot_general(middle, all_columns, (((1,), (1,)), ((), ())), preferred_...]
    all_to_all x2 -> x0, starting transfers between devices: 14.1 us -> none  [the longest x1 9.72 us: shards(): lax.all_to_all(rot_in, 'wide', split_axis=1, concat_axis=0, tiled=True)]
    unnamed x12 -> x4, local copies, waits for them, and re-layouts: 2.79 us -> 7.64 us
  transfers between devices with their start and end apart: 5 -> 0, of which waited for: 4 -> 0; matrix products, arithmetic and copies ran while one was open for 3% -> 0% of each run, Pallas kernels for 0% -> 0%
where the time goes in v1:
time: 159 us; the launch traced here: 158 us
  Pallas kernels  149 us (94%)
  local copies, waits for them, and re-layouts  7.64 us (5%)
    pallas_call x1, Pallas kernels, shards(): pl.pallas_call(kernel, out_shape=(tile, tile), in_specs=[vm] * 6 + [hbm]...  149 us
    unnamed x4, local copies, waits for them, and re-layouts  7.64 us

profile of v1, /device:TPU:1, one launch (start us, length us, event | category | flops | bytes accessed | tf_op | source)
XLA Modules:
  0.0 158.4 jit_solution(16455069949523315941)
XLA Ops:
  1.3 1.7 %copy.10.x_ref = bf16[256,320]{1,0:T(8,128)(2,1)} copy(bf16[256,320]{0,1:T(8,128)(2,1)} %param.8) | data formatting | bytes 327680 | tf_op args[0]
  3.0 1.7 %copy.11.g_ref = bf16[256,320]{1,0:T(8,128)(2,1)} copy(bf16[256,320]{0,1:T(8,128)(2,1)} %param.9) | data formatting | bytes 327680 | tf_op args[1]
  4.7 149.5 %shard_map.95 = (f32[320,640]{1,0:T(8,128)}, f32[320,640]{1,0:T(8,128)}) custom-call(bf16[256,320]{1,0:T(8,128)(2,1)} %copy.10.x_ref, bf16[256,320]{1,0:T(8,128)(2,1)} %copy.11.g_ref, s32[1,256]{1,0:T(1,128)} %bitcast.4, s32[1,2]{1,0:T(1,128)} %bitcast.5, f32[1,1]{1,0:T(1,128)} %bitcast.3.damp_ref, bf16[320,640]{1,0:T(8,128)(2,1)} %q_ref.1, ...), custom_call_target="tpu_custom_call" | custom-call | tf_op jit(solution)/shard_map/pallas_call | solution.py:389
  154.2 2.1 %copy.15 = f32[320,640]{1,0:T(8,128)} copy(f32[320,640]{1,0:T(8,128)} %get-tuple-element.4) | data formatting | bytes 1638400
  156.3 2.1 %copy.16 = f32[320,640]{1,0:T(8,128)} copy(f32[320,640]{1,0:T(8,128)} %get-tuple-element.5) | data formatting | bytes 1638400

commit v2 on v1

--- a/solution.py
+++ b/solution.py
@@ -15,13 +15,15 @@
 WB = 640
 SUB = 16
 GROWS = NB + 16
-NSEM = 192
+PARTS = ((0, 256), (256, 256), (512, 128))
+NSEM = 256
 
 
 def kernel(
-    x_ref, g_ref, ids_ref, cnt_ref, damp_ref, q_ref, bin_hbm, bout_hbm,
-    eig_ref, out_ref,
-    bout, incols, xw, pt, ps, rh, rf, ry, ryb, gt, rot, rotacc, sall, acc, mid, pb, eh, ef, ey, eyb,
+    ids_ref, cnt_ref, damp_ref, x_hbm, g_hbm, q_hbm, bin_hbm, bout_hbm,
+    eig_hbm, out_hbm,
+    xt, gtt, xv, gv, qv, bout, incols, xw, pt, ps, rh, rf, ry, ryb, gt, rot, rotacc, tall, acc, out,
+    scaled, pb, eh, ef, ey, eyb,
     ssem, rsem, lsem,
 ):
     w = lax.axis_index("wide")
@@ -57,16 +59,26 @@
         sent.append(copy)
         return copy
 
+    load_x = pltpu.make_async_copy(x_hbm, xt, lsem.at[2])
+    load_x.start()
+    load_g = pltpu.make_async_copy(g_hbm, gtt, lsem.at[3])
+    load_g.start()
+    load_q = pltpu.make_async_copy(q_hbm, qv, lsem.at[4])
     load_bout = pltpu.make_async_copy(bout_hbm, bout, lsem.at[0])
     load_bout.start()
     mine = pl.ds(pl.multiple_of(w * WB, 128), WB)
     load_cols = pltpu.make_async_copy(bin_hbm.at[:, mine], incols.at[n], lsem.at[1])
     load_cols.start()
+    load_q.start()
 
     barrier = pltpu.get_barrier_semaphore()
     others = [(w, (n + d) % 16) for d in range(1, 16)]
     for to in others + [zr, zl, yq, ynb]:
         pl.semaphore_signal(barrier, inc=1, device_id=to, device_id_type=MESH)
+    load_x.wait()
+    xv[...] = xt[...].astype(F32).T.astype(BF)
+    load_g.wait()
+    gv[...] = gtt[...].astype(F32).T.astype(BF)
     pl.semaphore_wait(barrier, len(others) + 4)
 
     class Gather:
@@ -146,7 +158,7 @@
             for d, (dx, part, to) in enumerate(((1, 1, self.right), (3, 0, self.left))):
                 self.one[y][d].wait_recv()
                 v = self.half(self.slot(dx, y), part)
-                v[...] = (v[...].astype(F32) + self.h[y, d].astype(F32)).astype(BF)
+                v[...] = (v[...].astype(F32) + self.h.at[y, d][...].astype(F32)).astype(BF)
                 copy = send(self.view(self.slot(dx, y)), self.f.at[y, d], to)
                 self.two[y] = self.two.get(y, ()) + (copy,)
 
@@ -154,7 +166,11 @@
             for copy in self.two[y]:
                 copy.wait_recv()
             own = self.view(self.slot(0, y))
-            return own[...].astype(F32) + self.f[y, 0].astype(F32) + self.f[y, 1].astype(F32)
+            return (
+                own[...].astype(F32)
+                + self.f.at[y, 0][...].astype(F32)
+                + self.f.at[y, 1][...].astype(F32)
+            )
 
         def third(self):
             self.fyb[...] = self.total(1).astype(BF)
@@ -175,14 +191,14 @@
     put_x = []
     for to in others:
         rows = pl.ds(pl.multiple_of(to[1] * SUB, SUB), SUB)
-        put_x.append(send(x_ref.at[rows], xw.at[w, n], to))
-    xw[w, n] = x_ref[pl.ds(pl.multiple_of(n * SUB, SUB), SUB), :]
+        put_x.append(send(xv.at[rows], xw.at[w, n], to))
+    xw[w, n] = xv[pl.ds(pl.multiple_of(n * SUB, SUB), SUB), :]
 
     load_bout.wait()
 
     def rotate_grad(c, _):
         at = pl.ds(pl.multiple_of(c * WB, 128), WB)
-        part = jnp.dot(g_ref[...], bout[:, at], preferred_element_type=F32).T
+        part = jnp.dot(gv[...], bout[:, at], preferred_element_type=F32).T
         pt[0, c] = part[:NB].astype(BF)
         pt[1, c] = part[NB:].astype(BF)
         return _
@@ -312,72 +328,152 @@
         return _
 
     lax.fori_loop(0, 8, fit, 0)
+    load_q.wait()
     eig = acc[...] * (1.0 / 16)
-    eig_ref[...] = eig
-    sall[n] = (q_ref[...].astype(F32) / (eig + damp_ref[...])).astype(BF)
-
-    sg = Gather(
-        lambda s: sall.at[s], lambda s, h: sall.at[s, pl.ds(160 * h, 160)],
-        nslot, xr, xl, yp, True,
-    )
-    sg.start()
-
-    def rotate_out(dx, dy, first=False):
-        c = cslot(dx, dy)
-        at = pl.ds(pl.multiple_of(c * WB, 128), WB)
-        part = jnp.dot(
-            bout[:, at], sall[pl.ds(2 * c, 2)].reshape(WB, WB), preferred_element_type=F32
-        )
-        acc[...] = part if first else acc[...] + part
-
-    sg.got_sib(0)
-    rotate_out(0, 0, True)
-    sg.near()
-    sg.got_sib(1)
-    rotate_out(3, 0)
-    sg.got_sib(2)
-    rotate_out(1, 0)
-    sg.across()
-    sg.far()
-    sg.got_sib(3)
-    rotate_out(0, 1)
-    sg.got_sib(4)
-    rotate_out(2, 0)
-    sg.across_near()
-    sg.got_sib(5)
-    rotate_out(3, 1)
-    sg.got_sib(6)
-    rotate_out(1, 1)
-    sg.across_far()
-    sg.got_sib(7)
-    rotate_out(2, 1)
-    mid[...] = acc[...].astype(BF)
-
-    def back(dz, dy):
-        s = wslot(dz, dy)
-        pb[s] = lax.dot_general(
-            mid[...], incols[pl.ds(2 * s, 2)].reshape(WB, WB), (((1,), (1,)), ((), ())),
-            preferred_element_type=F32,
+    acc[...] = eig
+    put_eig = pltpu.make_async_copy(acc, eig_hbm, lsem.at[5])
+    put_eig.start()
+    scaled[...] = (qv[...].astype(F32) / (eig + damp_ref[...])).astype(BF)
+
+    def back(s, at, wide):
+        pb[s, :, pl.ds(at, wide)] = lax.dot_general(
+            scaled[...], incols[pl.ds(2 * s, 2)].reshape(WB, WB)[at:at + wide],
+            (((1,), (1,)), ((), ())), preferred_element_type=F32,
         ).astype(BF)
 
-    es = Scatter(
-        lambda s: pb.at[s], lambda s, h: pb.at[s, pl.ds(160 * h, 160)],
-        wslot, zr, zl, yq, eh, ef, ey, eyb,
-    )
-    back(2, 1)
-    es.first(1)
-    back(2, 0)
-    es.first(0)
-    for dy in (1, 0):
-        for dz in (1, 3, 0):
-            back(dz, dy)
-    es.second(1)
-    es.second(0)
-    es.third()
-    out_ref[...] = es.fourth()
+    class Part:
+        def __init__(self, at, wide):
+            self.at, self.wide = at, wide
+            cols = pl.ds(at, wide)
+            self.cols = cols
+            self.es = Scatter(
+                lambda s: pb.at[s, :, cols], lambda s, h: pb.at[s, pl.ds(160 * h, 160), cols],
+                wslot, zr, zl, yq, eh.at[:, :, :, cols], ef.at[:, :, :, cols],
+                ey.at[:, cols], eyb.at[:, cols],
+            )
+            self.tg = Gather(
+                lambda s: tall.at[s, :, cols], lambda s, h: tall.at[s, pl.ds(160 * h, 160), cols],
+                nslot, xr, xl, yp, True,
+            )
+
+        def backs(self, slots):
+            for dz, dy in slots:
+                back(wslot(dz, dy), self.at, self.wide)
+
+        def begin(self):
+            for y in (1, 0):
+                self.backs([(2, y)])
+                self.es.first(y)
+
+        def rest(self):
+            self.backs([(dz, dy) for dy in (1, 0) for dz in (1, 3, 0)])
+
+        def gather(self):
+            tall[n, :, self.cols] = self.es.fourth().astype(BF)
+            self.tg.start()
+
+        def rotate_out(self, dx, dy, i):
+            self.tg.got_sib(i)
+            c = cslot(dx, dy)
+            rows = pl.ds(pl.multiple_of(c * WB, 128), WB)
+            part = jnp.dot(
+                bout[:, rows], tall[pl.ds(2 * c, 2), :, self.cols].reshape(WB, self.wide),
+                preferred_element_type=F32,
+            )
+            out[:, self.cols] = part if i == 0 else out[:, self.cols] + part
+
+        def near(self):
+            self.rotate_out(0, 0, 0)
+            self.tg.near()
+            self.rotate_out(3, 0, 1)
+            self.rotate_out(1, 0, 2)
+
+        def across(self):
+            self.tg.across()
+            self.tg.far()
+            self.rotate_out(0, 1, 3)
+            self.rotate_out(2, 0, 4)
+
+        def across_near(self):
+            self.tg.across_near()
+            self.rotate_out(3, 1, 5)
+            self.rotate_out(1, 1, 6)
+
+        def across_far(self):
+            self.tg.across_far()
+            self.rotate_out(2, 1, 7)
+
+    a, b, c = [Part(*p) for p in PARTS]
+    a.begin()
+    a.rest()
+    b.begin()
+    b.rest()
+    a.es.second(1)
+    a.es.second(0)
+    c.begin()
+    c.rest()
+    a.es.third()
+    b.es.second(1)
+    a.gather()
+    b.es.second(0)
+    c.es.second(1)
+    c.es.second(0)
+    b.es.third()
+    a.near()
+    b.gather()
+    a.across()
+    c.es.third()
+    c.gather()
+    b.near()
+    a.across_near()
+    b.across()
+    a.across_far()
+    c.near()
+    b.across_near()
+    c.across()
+    b.across_far()
+    c.across_near()
+    c.across_far()
+    put_out = pltpu.make_async_copy(out, out_hbm, lsem.at[6])
+    put_out.start()
+    put_eig.wait()
+    put_out.wait()
 
     for copy in sent:
         copy.wait_send()
+
+
+def pass_on(a_hbm, b_hbm, a_out, b_out, held, sem):
+    half = NB // 2
+    moves = []
+    for i, (src, dst) in enumerate(((a_hbm, a_out), (b_hbm, b_out))):
+        for h in range(2):
+            rows = pl.ds(h * half, half)
+            at = 2 * i + h
+            moves.append((
+                pltpu.make_async_copy(src.at[rows], held.at[at], sem.at[at, 0]),
+                pltpu.make_async_copy(held.at[at], dst.at[rows], sem.at[at, 1]),
+            ))
+    for take, _ in moves:
+        take.start()
+    for take, put in moves:
+        take.wait()
+        put.start()
+    for _, put in moves:
+        put.wait()
+
+
+def hand_on(a, b):
+    hbm = pl.BlockSpec(memory_space=pl.ANY)
+    return pl.pallas_call(
+        pass_on,
+        out_shape=(jax.ShapeDtypeStruct(a.shape, a.dtype), jax.ShapeDtypeStruct(b.shape, b.dtype)),
+        in_specs=[hbm, hbm],
+        out_specs=(hbm, hbm),
+        scratch_shapes=[
+            pltpu.VMEM((4, NB // 2, WB), F32), pltpu.SemaphoreType.DMA((4, 2)),
+        ],
+    )(a, b)
 
 
 def shards(
@@ -386,12 +482,17 @@
     vm = pl.BlockSpec(memory_space=pltpu.VMEM)
     hbm = pl.BlockSpec(memory_space=pl.ANY)
     tile = jax.ShapeDtypeStruct((NB, WB), F32)
-    return pl.pallas_call(
+    tiles = pl.pallas_call(
         kernel,
         out_shape=(tile, tile),
-        in_specs=[vm] * 6 + [hbm] * 2,
-        out_specs=(vm, vm),
+        in_specs=[vm] * 3 + [hbm] * 5,
+        out_specs=(hbm, hbm),
         scratch_shapes=[
+            pltpu.VMEM((NB, TOK), BF),
+            pltpu.VMEM((NB, TOK), BF),
+            pltpu.VMEM((TOK, NB), BF),
+            pltpu.VMEM((TOK, NB), BF),
+            pltpu.VMEM((NB, WB), BF),
             pltpu.VMEM((NB, D), BF),
             pltpu.VMEM((16, NB, WB), BF),
             pltpu.VMEM((8, 16, SUB, NB), BF),
@@ -406,6 +507,7 @@
             pltpu.VMEM((8 * SUB, WB), F32),
             pltpu.VMEM((16, NB, WB), BF),
             pltpu.VMEM((NB, WB), F32),
+            pltpu.VMEM((NB, WB), F32),
             pltpu.VMEM((NB, WB), BF),
             pltpu.VMEM((8, NB, WB), BF),
             pltpu.VMEM((2, 2, NB // 2, WB), BF),
@@ -414,15 +516,16 @@
             pltpu.VMEM((NB, WB), BF),
             pltpu.SemaphoreType.DMA((NSEM,)),
             pltpu.SemaphoreType.DMA((NSEM,)),
-            pltpu.SemaphoreType.DMA((2,)),
+            pltpu.SemaphoreType.DMA((7,)),
         ],
         compiler_params=pltpu.CompilerParams(
             collective_id=0, has_side_effects=True, vmem_limit_bytes=60 * 1024 * 1024
         ),
     )(
-        saved_inputs, out_grads, seq_ids.reshape(1, -1), seq_counts.reshape(1, -1),
-        damping.reshape(1, 1), query_rotated, basis_in, basis_out,
-    )
+        seq_ids.reshape(1, -1), seq_counts.reshape(1, -1), damping.reshape(1, 1),
+        saved_inputs.T, out_grads.T, query_rotated, basis_in, basis_out,
+    )
+    return hand_on(*tiles)
 
 
 def solution(mesh):

time: 159 us -> 147 us (0.925)
  local copies, waits for them, and re-layouts: 7.64 us -> 0 us
  Pallas kernels: 149 us -> 145 us
    unnamed x4 -> x0, local copies, waits for them, and re-layouts: 7.64 us -> none
    pallas_call x1 -> x2, Pallas kernels: 149 us -> 145 us  [the longest x1 143 us: shards(): pl.pallas_call(kernel, out_shape=(tile, tile), in_specs=[vm] * 3 + [hbm]...]
where the time goes in v2:
time: 147 us
  Pallas kernels  145 us (99%)
    pallas_call x1, Pallas kernels, shards(): pl.pallas_call(kernel, out_shape=(tile, tile), in_specs=[vm] * 3 + [hbm]...  143 us

profile of v2, /device:TPU:1, one launch (start us, length us, event | category | flops | bytes accessed | tf_op | source)
XLA Modules:
  0.0 146.8 jit_solution(10136207443440766500)
XLA Ops:
  1.3 143.1 %shard_map.95 = (f32[320,640]{1,0:T(8,128)}, f32[320,640]{1,0:T(8,128)}) custom-call(s32[1,256]{1,0:T(1,128)} %bitcast.8, s32[1,2]{1,0:T(1,128)} %bitcast.9, f32[1,1]{1,0:T(1,128)} %bitcast.5.damp_ref, bf16[320,256]{1,0:T(8,128)(2,1)} %bitcast.6, bf16[320,256]{1,0:T(8,128)(2,1)} %bitcast.7, bf16[320,640]{1,0:T(8,128)(2,1)} %q_hbm.1, ...), custom_call_target="tpu_custom_call" | custom-call | tf_op jit(solution)/shard_map/pallas_call | solution.py:485
  144.4 2.2 %shard_map.96 = (f32[320,640]{1,0:T(8,128)}, f32[320,640]{1,0:T(8,128)}) custom-call(f32[320,640]{1,0:T(8,128)} %get-tuple-element.4.a_hbm, f32[320,640]{1,0:T(8,128)} %get-tuple-element.5.b_hbm), custom_call_target="tpu_custom_call" | custom-call | tf_op jit(solution)/shard_map/pallas_call | solution.py:468

commit v3 on v2

--- a/solution.py
+++ b/solution.py
@@ -16,13 +16,24 @@
 SUB = 16
 GROWS = NB + 16
 PARTS = ((0, 256), (256, 256), (512, 128))
-NSEM = 256
+ORDER = (
+    (0, 0), (1, 10), (0, 1), (1, 11), (0, 2), (1, 12), (2, 10), (0, 3), (1, 1),
+    (2, 11), (2, 12), (1, 2), (0, 4), (1, 3), (0, 5), (0, 20), (2, 1), (2, 2),
+    (0, 6), (0, 7), (1, 4), (0, 21), (2, 3), (2, 4), (1, 5), (0, 8), (1, 6),
+    (1, 7), (1, 20), (0, 22), (2, 5), (0, 9), (2, 6), (2, 7), (1, 8), (1, 21),
+    (0, 23), (2, 20), (1, 22), (2, 8), (1, 9), (2, 21), (1, 23), (2, 9), (2, 22),
+    (2, 23),
+)
+NEAR = ((1, 1), (3, 1), (0, 1), (1, 0), (3, 0), (0, 0))
+ARRIVAL = ((0, 0), (3, 0), (1, 0), (0, 1), (2, 0), (3, 1), (1, 1), (2, 1))
+HALVES = ((0, 384), (384, 256))
+NSEM = 384
 
 
 def kernel(
     ids_ref, cnt_ref, damp_ref, x_hbm, g_hbm, q_hbm, bin_hbm, bout_hbm,
     eig_hbm, out_hbm,
-    xt, gtt, xv, gv, qv, bout, incols, xw, pt, ps, rh, rf, ry, ryb, gt, rot, rotacc, tall, acc, out,
+    xt, gtt, xv, gv, qv, bout, incols, xw, pt, ps, rh, rf, ry, ryb, gt, rot0, rot1, rotacc, tall, acc, out,
     scaled, pb, eh, ef, ey, eyb,
     ssem, rsem, lsem,
 ):
@@ -82,9 +93,10 @@
     pl.semaphore_wait(barrier, len(others) + 4)
 
     class Gather:
-        def __init__(self, view, half, slot, right, left, part, to_sib):
+        def __init__(self, view, half, slot, right, left, part, to_sib, far_to=None):
             self.view, self.half, self.slot = view, half, slot
             self.right, self.left, self.part, self.to_sib = right, left, part, to_sib
+            self.far_to = far_to
             self.sibs = []
 
         def fwd(self, dx, dy):
@@ -122,19 +134,26 @@
         def far(self):
             self.fr.wait_recv()
             self.fl.wait_recv()
+            if self.far_to is not None:
+                self.pf = self.hop(self.view(self.slot(2, 0)), self.far_to)
             self.fwd(2, 0)
 
         def across_near(self):
             self.pr.wait_recv()
-            self.pfr = self.hop(self.half(self.slot(3, 1), 0), self.right)
+            if self.far_to is None:
+                self.pfr = self.hop(self.half(self.slot(3, 1), 0), self.right)
             self.fwd(3, 1)
             self.pl.wait_recv()
-            self.pfl = self.hop(self.half(self.slot(1, 1), 1), self.left)
+            if self.far_to is None:
+                self.pfl = self.hop(self.half(self.slot(1, 1), 1), self.left)
             self.fwd(1, 1)
 
         def across_far(self):
-            self.pfr.wait_recv()
-            self.pfl.wait_recv()
+            if self.far_to is None:
+                self.pfr.wait_recv()
+                self.pfl.wait_recv()
+            else:
+                self.pf.wait_recv()
             self.fwd(2, 1)
 
         def got_sib(self, i):
@@ -181,17 +200,70 @@
             self.last.wait_recv()
             return t + self.fy[...].astype(F32)
 
-    theirs = pl.ds(pl.multiple_of(wslot(0, 1) * WB, 128), WB)
-    cols = Gather(
-        lambda s: incols.at[s], lambda s, h: incols.at[s, pl.ds(160 * h, 160)],
-        nslot, xr, xl, ynb, True,
-    )
-    cols.start(bin_hbm.at[:, mine], bin_hbm.at[:, theirs])
+    def rows_of(s):
+        return pl.ds(pl.multiple_of(s * SUB, SUB), SUB)
+
+    class Half:
+        def __init__(self, at, wide, rot):
+            self.at, self.wide, self.rot = at, wide, rot
+            self.cols = cols = pl.ds(at, wide)
+            self.cg = Gather(
+                lambda s: incols.at[s, :, cols],
+                lambda s, h: incols.at[s, pl.ds(160 * h, 160), cols],
+                nslot, xr, xl, ynb, True, yp,
+            )
+            self.rg = Gather(
+                lambda s: rot.at[:, rows_of(s)],
+                lambda s, h: rot.at[pl.ds(4 * h, 4), rows_of(s)],
+                nslot, xr, xl, yp, True,
+            )
+
+        def start(self):
+            def of(s):
+                return bin_hbm.at[:, pl.ds(pl.multiple_of(s * WB + self.at, 128), self.wide)]
+
+            self.cg.start(of(w), of(wslot(0, 1)))
+
+        def rotate_in(self, dx, dy, i):
+            self.cg.got_sib(i)
+            total = None
+            for core in range(2):
+                s = cslot(dx, dy) * 2 + core
+                part = jnp.dot(
+                    xw[:, s].reshape(8 * SUB, NB), incols[s, :, self.cols],
+                    preferred_element_type=F32,
+                )
+                total = part if total is None else total + part
+            rotacc[:, self.cols] = total if i == 0 else rotacc[:, self.cols] + total
+
+        def spread(self):
+            self.rot[:, rows_of(n)] = (
+                rotacc[:, self.cols].astype(BF).reshape(8, SUB, self.wide)
+            )
+            self.rg.start()
+
+        def fit(self):
+            acc[:, self.cols] = jnp.zeros((NB, self.wide), F32)
+
+            def block(b, _):
+                grad = gt[b, :NB]
+                mask = gt[b, NB:NB + 1]
+                one = grad * mask
+                rows = self.rot[b]
+                p = jnp.dot(one, rows, preferred_element_type=F32)
+                r = jnp.dot(grad - one, rows, preferred_element_type=F32)
+                acc[:, self.cols] += p * p + r * r
+                return _
+
+            lax.fori_loop(0, 8, block, 0)
+
+    p0, p1 = [Half(*h, rot) for h, rot in zip(HALVES, (rot0, rot1))]
 
     put_x = []
     for to in others:
         rows = pl.ds(pl.multiple_of(to[1] * SUB, SUB), SUB)
         put_x.append(send(xv.at[rows], xw.at[w, n], to))
+    p0.start()
     xw[w, n] = xv[pl.ds(pl.multiple_of(n * SUB, SUB), SUB), :]
 
     load_bout.wait()
@@ -205,13 +277,6 @@
 
     lax.fori_loop(0, 8, rotate_grad, 0)
     swap = send(pt.at[1 - k], ps, sib)
-
-    for copy in put_x:
-        copy.wait_recv()
-    xg = Gather(
-        lambda s: xw.at[s], lambda s, h: xw.at[s, pl.ds(8 * h, 8)], wslot, zr, zl, yq, False
-    )
-    xg.start()
 
     swap.wait_recv()
     grads = Scatter(
@@ -231,31 +296,28 @@
         for dx in (1, 3, 0):
             both(dx, dy)
 
-    cols.near()
+    for copy in put_x:
+        copy.wait_recv()
+    xg = Gather(
+        lambda s: xw.at[s], lambda s, h: xw.at[s, pl.ds(8 * h, 8)], wslot, zr, zl, yq, False
+    )
+    xg.start()
+    p0.cg.near()
     xg.near()
     xg.across()
     grads.second(1)
     grads.second(0)
-    cols.across()
+    p0.cg.across()
+    p0.cg.far()
+    p1.start()
     xg.far()
     xg.across_near()
     grads.third()
     xg.across_far()
     load_cols.wait()
-
-    def rotate_in(dx, dy, first=False):
-        total = None
-        for core in range(2):
-            s = cslot(dx, dy) * 2 + core
-            part = jnp.dot(
-                xw[:, s].reshape(8 * SUB, NB), incols[s], preferred_element_type=F32
-            )
-            total = part if total is None else total + part
-        rotacc[...] = total if first else rotacc[...] + total
-
-    cols.got_sib(0)
-    rotate_in(0, 0, True)
-    cols.far()
+    p0.rotate_in(0, 0, 0)
+    p0.rotate_in(3, 0, 1)
+    p0.rotate_in(1, 0, 2)
     rotg = grads.fourth()
 
     is_first = ids_ref[...] == 2 * w
@@ -272,62 +334,49 @@
     )
     gg.start()
 
-    cols.got_sib(1)
-    rotate_in(3, 0)
-    cols.got_sib(2)
-    rotate_in(1, 0)
-    cols.across_near()
-    cols.got_sib(3)
-    rotate_in(0, 1)
-    cols.got_sib(4)
-    rotate_in(2, 0)
+    p0.rotate_in(0, 1, 3)
+    p0.rotate_in(2, 0, 4)
+    p0.cg.across_near()
+    p0.rotate_in(3, 1, 5)
+    p0.rotate_in(1, 1, 6)
+    p1.cg.near()
+    p0.cg.across_far()
+    p0.rotate_in(2, 1, 7)
+    p0.spread()
+    p1.cg.across()
+    p1.rotate_in(0, 0, 0)
+    p1.rotate_in(3, 0, 1)
+    p1.rotate_in(1, 0, 2)
+    p1.cg.far()
     gg.near()
-    cols.got_sib(5)
-    rotate_in(3, 1)
-    cols.got_sib(6)
-    rotate_in(1, 1)
-    cols.across_far()
-    cols.got_sib(7)
-    rotate_in(2, 1)
-
-    rot[:, pl.ds(pl.multiple_of(n * SUB, SUB), SUB), :] = (
-        rotacc[...].astype(BF).reshape(8, SUB, WB)
-    )
-
-    def rows_of(s):
-        return pl.ds(pl.multiple_of(s * SUB, SUB), SUB)
-
-    rg = Gather(
-        lambda s: rot.at[:, rows_of(s)],
-        lambda s, h: rot.at[pl.ds(4 * h, 4), rows_of(s)],
-        nslot, xr, xl, yp, True,
-    )
-    rg.start()
+    p0.rg.near()
+    p1.rotate_in(0, 1, 3)
+    p1.rotate_in(2, 0, 4)
+    p1.cg.across_near()
+    p1.rotate_in(3, 1, 5)
+    p1.rotate_in(1, 1, 6)
+    p0.rg.across()
+    p0.rg.far()
     gg.across()
-    rg.near()
-    rg.across()
+    p1.cg.across_far()
+    p1.rotate_in(2, 1, 7)
+    p1.spread()
+    p0.rg.across_near()
     gg.far()
     gg.across_near()
-    rg.far()
-    rg.across_near()
+    p0.rg.across_far()
+    p1.rg.near()
     gg.across_far()
-    rg.across_far()
+    p1.rg.across()
     for i in range(8):
-        rg.got_sib(i)
-
-    acc[...] = jnp.zeros_like(acc)
-
-    def fit(b, _):
-        grad = gt[b, :NB]
-        mask = gt[b, NB:NB + 1]
-        one = grad * mask
-        rows = rot[b]
-        p = jnp.dot(one, rows, preferred_element_type=F32)
-        r = jnp.dot(grad - one, rows, preferred_element_type=F32)
-        acc[...] += p * p + r * r
-        return _
-
-    lax.fori_loop(0, 8, fit, 0)
+        p0.rg.got_sib(i)
+    p0.fit()
+    p1.rg.far()
+    p1.rg.across_near()
+    p1.rg.across_far()
+    for i in range(8):
+        p1.rg.got_sib(i)
+    p1.fit()
     load_q.wait()
     eig = acc[...] * (1.0 / 16)
     acc[...] = eig
@@ -360,14 +409,6 @@
             for dz, dy in slots:
                 back(wslot(dz, dy), self.at, self.wide)
 
-        def begin(self):
-            for y in (1, 0):
-                self.backs([(2, y)])
-                self.es.first(y)
-
-        def rest(self):
-            self.backs([(dz, dy) for dy in (1, 0) for dz in (1, 3, 0)])
-
         def gather(self):
             tall[n, :, self.cols] = self.es.fourth().astype(BF)
             self.tg.start()
@@ -382,58 +423,32 @@
             )
             out[:, self.cols] = part if i == 0 else out[:, self.cols] + part
 
-        def near(self):
-            self.rotate_out(0, 0, 0)
-            self.tg.near()
-            self.rotate_out(3, 0, 1)
-            self.rotate_out(1, 0, 2)
-
-        def across(self):
-            self.tg.across()
-            self.tg.far()
-            self.rotate_out(0, 1, 3)
-            self.rotate_out(2, 0, 4)
-
-        def across_near(self):
-            self.tg.across_near()
-            self.rotate_out(3, 1, 5)
-            self.rotate_out(1, 1, 6)
-
-        def across_far(self):
-            self.tg.across_far()
-            self.rotate_out(2, 1, 7)
-
-    a, b, c = [Part(*p) for p in PARTS]
-    a.begin()
-    a.rest()
-    b.begin()
-    b.rest()
-    a.es.second(1)
-    a.es.second(0)
-    c.begin()
-    c.rest()
-    a.es.third()
-    b.es.second(1)
-    a.gather()
-    b.es.second(0)
-    c.es.second(1)
-    c.es.second(0)
-    b.es.third()
-    a.near()
-    b.gather()
-    a.across()
-    c.es.third()
-    c.gather()
-    b.near()
-    a.across_near()
-    b.across()
-    a.across_far()
-    c.near()
-    b.across_near()
-    c.across()
-    b.across_far()
-    c.across_near()
-    c.across_far()
+        def step(self, k):
+            if k == 0:
+                for y in (1, 0):
+                    self.backs([(2, y)])
+                    self.es.first(y)
+                self.backs(NEAR)
+            elif k == 10:
+                self.backs(((2, 1), (2, 0)) + NEAR)
+            elif k in (11, 12):
+                self.es.first(12 - k)
+            elif k in (1, 2):
+                self.es.second(2 - k)
+            elif k == 3:
+                self.es.third()
+            elif k == 4:
+                self.gather()
+            elif k < 10:
+                (self.tg.near, self.tg.across, self.tg.far, self.tg.across_near,
+                 self.tg.across_far)[k - 5]()
+            else:
+                for i in ((0, 1, 2), (3, 4), (5, 6), (7,))[k - 20]:
+                    self.rotate_out(*ARRIVAL[i], i)
+
+    parts = [Part(*p) for p in PARTS]
+    for i, what in ORDER:
+        parts[i].step(what)
     put_out = pltpu.make_async_copy(out, out_hbm, lsem.at[6])
     put_out.start()
     put_eig.wait()
@@ -503,7 +518,8 @@
             pltpu.VMEM((NB, TOK), BF),
             pltpu.VMEM((NB, TOK), BF),
             pltpu.VMEM((8, GROWS, TOK), BF),
-            pltpu.VMEM((8, TOK, WB), BF),
+            pltpu.VMEM((8, TOK, HALVES[0][1]), BF),
+            pltpu.VMEM((8, TOK, HALVES[1][1]), BF),
             pltpu.VMEM((8 * SUB, WB), F32),
             pltpu.VMEM((16, NB, WB), BF),
             pltpu.VMEM((NB, WB), F32),

time: 147 us -> 139 us (0.946)
  Pallas kernels: 145 us -> 138 us
    pallas_call x1, Pallas kernels: 143 us -> 135 us  [shards(): pl.pallas_call(kernel, out_shape=(tile, tile), in_specs=[vm] * 3 + [hbm]...]
where the time goes in v3:
time: 139 us
  Pallas kernels  138 us (99%)
  between operations  1.45 us (1%)
    pallas_call x1, Pallas kernels, shards(): pl.pallas_call(kernel, out_shape=(tile, tile), in_specs=[vm] * 3 + [hbm]...  135 us

profile of v3, /device:TPU:1, one launch (start us, length us, event | category | flops | bytes accessed | tf_op | source)
XLA Modules:
  0.0 139.1 jit_solution(6937571104511887926)
XLA Ops:
  1.3 135.4 %shard_map.95 = (f32[320,640]{1,0:T(8,128)}, f32[320,640]{1,0:T(8,128)}) custom-call(s32[1,256]{1,0:T(1,128)} %bitcast.8, s32[1,2]{1,0:T(1,128)} %bitcast.9, f32[1,1]{1,0:T(1,128)} %bitcast.5.damp_ref, bf16[320,256]{1,0:T(8,128)(2,1)} %bitcast.6, bf16[320,256]{1,0:T(8,128)(2,1)} %bitcast.7, bf16[320,640]{1,0:T(8,128)(2,1)} %q_hbm.1, ...), custom_call_target="tpu_custom_call" | custom-call | tf_op jit(solution)/shard_map/pallas_call | solution.py:500
  136.7 2.2 %shard_map.96 = (f32[320,640]{1,0:T(8,128)}, f32[320,640]{1,0:T(8,128)}) custom-call(f32[320,640]{1,0:T(8,128)} %get-tuple-element.4.a_hbm, f32[320,640]{1,0:T(8,128)} %get-tuple-element.5.b_hbm), custom_call_target="tpu_custom_call" | custom-call | tf_op jit(solution)/shard_map/pallas_call | solution.py:483

commit v4 on v3

--- a/solution.py
+++ b/solution.py
@@ -215,7 +215,7 @@
             self.rg = Gather(
                 lambda s: rot.at[:, rows_of(s)],
                 lambda s, h: rot.at[pl.ds(4 * h, 4), rows_of(s)],
-                nslot, xr, xl, yp, True,
+                nslot, xr, xl, yp, True, yp,
             )
 
         def start(self):

time: 139 us -> 139 us (level)
  no operation moved by 1% of the time
where the time goes in v4:
time: 139 us
  Pallas kernels  137 us (99%)
  between operations  1.45 us (1%)
    pallas_call x1, Pallas kernels, shards(): pl.pallas_call(kernel, out_shape=(tile, tile), in_specs=[vm] * 3 + [hbm]...  135 us

profile of v4, /device:TPU:1, one launch (start us, length us, event | category | flops | bytes accessed | tf_op | source)
XLA Modules:
  0.0 138.9 jit_solution(2180914351825752565)
XLA Ops:
  1.3 135.3 %shard_map.95 = (f32[320,640]{1,0:T(8,128)}, f32[320,640]{1,0:T(8,128)}) custom-call(s32[1,256]{1,0:T(1,128)} %bitcast.8, s32[1,2]{1,0:T(1,128)} %bitcast.9, f32[1,1]{1,0:T(1,128)} %bitcast.5.damp_ref, bf16[320,256]{1,0:T(8,128)(2,1)} %bitcast.6, bf16[320,256]{1,0:T(8,128)(2,1)} %bitcast.7, bf16[320,640]{1,0:T(8,128)(2,1)} %q_hbm.1, ...), custom_call_target="tpu_custom_call" | custom-call | tf_op jit(solution)/shard_map/pallas_call | solution.py:500
  136.6 2.2 %shard_map.96 = (f32[320,640]{1,0:T(8,128)}, f32[320,640]{1,0:T(8,128)}) custom-call(f32[320,640]{1,0:T(8,128)} %get-tuple-element.4.a_hbm, f32[320,640]{1,0:T(8,128)} %get-tuple-element.5.b_hbm), custom_call_target="tpu_custom_call" | custom-call | tf_op jit(solution)/shard_map/pallas_call | solution.py:483
